TPU v7x, 32 devices: a whole 2x2x4 slice. The times are simulated.
32 devices in a mesh: ka: 8 (over z, core), band: 4 (over y, x).
Axes of the slice: x: 2, y: 2, z: 4, core: 2. Of those that a mesh axis runs over, the one named last changes fastest.
Arguments:
- occ_rows: bfloat16 [8, 2048, 128], P('ka', 'band'), may hold values from -0.5 to 0.5
- vir_rows: bfloat16 [8, 2048, 896], P('ka', 'band'), may hold values from -0.1875 to 0.1875
- trial_vectors: float32 [8, 2, 128, 896], P('ka', None, None, 'band'), may hold values from -6 to 6
- occ_energy: float32 [8, 128], P('ka'), may hold values from -1.2 to -0.3
- vir_energy: float32 [8, 896], P('ka', 'band'), may hold values from 0.1 to 1.5
- coulomb: bfloat16 [2048, 2048], P('band'), may hold values from -0.09375 to 0.09375
- exch_kernel: bfloat16 [8, 2048, 2048], P(None, 'band'), as said below
- minus_table: int32 [8, 8], replicated, may hold values from 0 to 7, as said below
Outputs:
- sigma_vectors: float32 [8, 2, 128, 896], P('ka', None, None, 'band')
Inputs may be any that keep to these rules, and one draw needn't show every extreme that they name: minus_table[k, q] is the k-point k - q on a group of 8 k-points: every row and every column holds each index once, and one q gives minus_table[k, q] == k for every k. Each exch_kernel[q] is symmetric.
All inputs are finite; a program needn't handle non-finite values.
Results may differ from a plain program's by a relative error of at most 0.0051.
Values may be sent and summed in bfloat16 or wider, within the bound.
No kernel may reach another device: no remote copies, remote signals or barrier semaphores. Data moves between devices by JAX's collectives and lax.ppermute only.
A program may use at most 128 MiB of HBM per device.

v0:
```python
import jax
import jax.numpy as jnp
from jax import lax
from jax.experimental import pallas as pl
from jax.experimental.pallas import tpu as pltpu
from jax.sharding import PartitionSpec as P


MIB = 1024 * 1024
ROWS = 16
EXTRA = 16


def spread_kernel(trial_ref, out_ref):
    copies = out_ref.shape[0]
    vectors, _, nocc = trial_ref.shape
    for v in range(vectors):
        rounded = trial_ref[v].astype(jnp.bfloat16)
        for b in range(copies):
            out_ref[b, :, v * nocc : (v + 1) * nocc] = rounded


def spread(trial, copies):
    vectors, virtual, nocc = trial.shape
    return pl.pallas_call(
        spread_kernel,
        out_shape=jax.ShapeDtypeStruct((copies, virtual, vectors * nocc), jnp.bfloat16),
        compiler_params=pltpu.CompilerParams(vmem_limit_bytes=12 * MIB),
    )(trial)


def prepare_kernel(vir_ref, trial_ref, occ_hbm, out_ref, occ_ref, arrived):
    copy = pltpu.make_async_copy(occ_hbm, occ_ref, arrived)
    copy.start()
    kpoints, _, width = out_ref.shape
    rows, nocc = occ_ref.shape
    points = rows // kpoints
    vectors = width // nocc
    mapped = jnp.dot(vir_ref[...], trial_ref[...], preferred_element_type=jnp.float32)
    mapped = mapped.astype(jnp.bfloat16)
    copy.wait()
    occ = occ_ref[...].astype(jnp.float32)
    ones = jnp.ones((EXTRA, nocc), jnp.bfloat16)
    place = lax.broadcasted_iota(jnp.int32, (EXTRA, width), 0)
    extra = jnp.zeros((EXTRA, width), jnp.float32)
    index = 0
    over_lanes = (((1,), (1,)), ((), ()))
    for v in range(vectors):
        terms = mapped[:, v * nocc : (v + 1) * nocc].astype(jnp.float32) * occ
        high = terms.astype(jnp.bfloat16)
        low = (terms - high.astype(jnp.float32)).astype(jnp.bfloat16)
        summed = lax.dot_general(ones, high, over_lanes, preferred_element_type=jnp.float32)
        summed += lax.dot_general(ones, low, over_lanes, preferred_element_type=jnp.float32)
        for start in range(0, rows, width):
            piece = summed[:, start : start + width]
            high_piece = piece.astype(jnp.bfloat16).astype(jnp.float32)
            extra = jnp.where(place == index, high_piece, extra)
            extra = jnp.where(place == index + EXTRA // 2, piece - high_piece, extra)
            index += 1
    extra = extra.astype(jnp.bfloat16)
    for j in range(kpoints):
        out_ref[j, :points] = mapped[j * points : (j + 1) * points]
        out_ref[j, points:] = extra


def prepare(kpoints, vir_own, trial_full, occ_own):
    rows = occ_own.shape[0]
    width = trial_full.shape[1]
    return pl.pallas_call(
        prepare_kernel,
        in_specs=[pl.BlockSpec(memory_space=pltpu.VMEM)] * 2
        + [pl.BlockSpec(memory_space=pl.ANY)],
        out_specs=pl.BlockSpec(memory_space=pltpu.VMEM),
        scratch_shapes=[pltpu.VMEM(occ_own.shape, jnp.bfloat16), pltpu.SemaphoreType.DMA],
        out_shape=jax.ShapeDtypeStruct((kpoints, rows // kpoints + EXTRA, width), jnp.bfloat16),
        compiler_params=pltpu.CompilerParams(vmem_limit_bytes=12 * MIB),
        cost_estimate=pl.CostEstimate(
            flops=2 * vir_own.size * width, bytes_accessed=2 * vir_own.size, transcendentals=0
        ),
    )(vir_own, trial_full, occ_own)


def exchange_kernel(y_ref, table_hbm, exch_hbm, *refs):
    z_ref, table_ref, where_ref, occ_ref, exch_ref, pair_ref, scr_ref, acc_ref, arrived, known = refs[-10:]
    blocks = refs[:-10]
    count, kpoints, points, rows = exch_ref.shape
    tile, nocc = pair_ref.shape[2], occ_ref.shape[4]
    vectors = z_ref.shape[2] // nocc
    own = lax.axis_index("ka").astype(jnp.int32)
    band = lax.axis_index("band").astype(jnp.int32)

    table_copy = pltpu.make_async_copy(table_hbm, table_ref, known)
    table_copy.start()
    copies = []
    mine = pl.ds(pl.multiple_of(own * points, points), points)
    for c in range(count):
        first = pl.multiple_of((band ^ c) * rows, rows)
        copies.append(
            [
                pltpu.make_async_copy(blocks[2 * c], occ_ref.at[c, 0], arrived.at[c, 0]),
                pltpu.make_async_copy(blocks[2 * c + 1], occ_ref.at[c, 1], arrived.at[c, 1]),
                pltpu.make_async_copy(
                    exch_hbm.at[:, mine, pl.ds(first, rows)], exch_ref.at[c], arrived.at[c, 2]
                ),
            ]
        )
    for group in copies:
        for copy in group:
            copy.start()
    acc_ref[...] = jnp.zeros_like(acc_ref)
    table_copy.wait()
    for k in range(kpoints):
        for q in range(kpoints):
            where_ref[k, q] = table_ref[own ^ k, q] ^ own

    for c in range(count):
        for copy in copies[c]:
            copy.wait()

        @pl.loop(0, rows // tile)
        def _(t):
            here = pl.ds(pl.multiple_of(t * tile, tile), tile)
            for s in range(kpoints):
                y_here = y_ref[own ^ s]
                stacked = jnp.concatenate(
                    [y_here[:points, v * nocc : (v + 1) * nocc] for v in range(vectors)], axis=0
                )
                pair_ref[s] = lax.dot_general(
                    stacked,
                    occ_ref[c, s % 2, s // 2, here],
                    (((1,), (1,)), ((), ())),
                    preferred_element_type=jnp.float32,
                )
            for r in range(0, points, ROWS):
                kern = [
                    exch_ref[c, q, r : r + ROWS, here].astype(jnp.float32) for q in range(kpoints)
                ]
                for k in range(kpoints):
                    total = [None] * vectors
                    for q in range(kpoints):
                        source = where_ref[k, q]
                        for v in range(vectors):
                            at = v * points + r
                            term = pair_ref[source, at : at + ROWS] * kern[q]
                            total[v] = term if total[v] is None else total[v] + term
                    for v in range(vectors):
                        at = v * points + r
                        scr_ref[k, at : at + ROWS] = total[v].astype(jnp.bfloat16)
            for s in range(kpoints):
                acc_ref[s] += jnp.dot(
                    scr_ref[s],
                    occ_ref[c, s % 2, s // 2, here],
                    preferred_element_type=jnp.float32,
                )

    for s in range(kpoints):
        for v in range(vectors):
            z_ref[own ^ s, :, v * nocc : (v + 1) * nocc] = acc_ref[
                s, v * points : (v + 1) * points
            ].astype(z_ref.dtype)


def exchange(table, y_all, blocks, exch):
    kpoints, _, width = y_all.shape
    half, rows, nocc = blocks[0].shape
    chunks = len(blocks) // 2
    points = rows // kpoints
    tile = min(256, rows)
    stacked = points * width // nocc
    held = pl.BlockSpec(memory_space=pltpu.VMEM)
    flops = 4 * kpoints * stacked * chunks * rows * nocc
    return pl.pallas_call(
        exchange_kernel,
        in_specs=[held] + [pl.BlockSpec(memory_space=pl.ANY)] * (2 + len(blocks)),
        out_specs=held,
        scratch_shapes=[
            pltpu.SMEM((kpoints, kpoints), jnp.int32),
            pltpu.SMEM((kpoints, kpoints), jnp.int32),
            pltpu.VMEM((chunks, 2, half, rows, nocc), jnp.bfloat16),
            pltpu.VMEM((chunks, kpoints, points, rows), jnp.bfloat16),
            pltpu.VMEM((kpoints, stacked, tile), jnp.float32),
            pltpu.VMEM((kpoints, stacked, tile), jnp.bfloat16),
            pltpu.VMEM((kpoints, stacked, nocc), jnp.float32),
            pltpu.SemaphoreType.DMA((chunks, 3)),
            pltpu.SemaphoreType.DMA,
        ],
        out_shape=jax.ShapeDtypeStruct((kpoints, points, width), jnp.bfloat16),
        cost_estimate=pl.CostEstimate(
            flops=16 * flops,
            bytes_accessed=2 * kpoints * chunks * rows * (nocc + points),
            transcendentals=0,
        ),
    )(y_all, table, exch, *blocks)


def density_kernel(y_ref, out_ref):
    vectors, rows = out_ref.shape
    width = y_ref.shape[2]
    pieces = rows // width
    points = y_ref.shape[1] - EXTRA
    halves = jnp.sum(y_ref[:, points:].astype(jnp.float32), axis=0)
    halves = halves[: EXTRA // 2] + halves[EXTRA // 2 :]
    out_ref[...] = jnp.concatenate(
        [
            jnp.concatenate(
                [halves[v * pieces + h : v * pieces + h + 1] for h in range(pieces)], axis=1
            )
            for v in range(vectors)
        ],
        axis=0,
    ).astype(jnp.bfloat16)


def summed_density(vectors, rows, y_all):
    return pl.pallas_call(
        density_kernel,
        out_shape=jax.ShapeDtypeStruct((vectors, rows), jnp.bfloat16),
        compiler_params=pltpu.CompilerParams(vmem_limit_bytes=4 * MIB),
    )(y_all)


def potential_kernel(coulomb_ref, occ_ref, *refs):
    density_refs, out_ref = refs[:-1], refs[-1]
    vectors, rows = density_refs[0].shape
    nocc = occ_ref.shape[1]
    band = lax.axis_index("band").astype(jnp.int32)
    total = None
    for b, density_ref in enumerate(density_refs):
        density = density_ref[...].astype(jnp.float32)
        first = pl.multiple_of((band ^ b) * rows, rows)
        spread = jnp.concatenate(
            [jnp.broadcast_to(density[v : v + 1], (nocc, rows)) for v in range(vectors)], axis=0
        ).astype(jnp.bfloat16)
        term = lax.dot_general(
            coulomb_ref[:, pl.ds(first, rows)],
            spread,
            (((1,), (1,)), ((), ())),
            preferred_element_type=jnp.float32,
        )
        total = term if total is None else total + term
    occ = 2.0 * occ_ref[...].astype(jnp.float32)
    for v in range(vectors):
        out_ref[:, v * nocc : (v + 1) * nocc] = total[:, v * nocc : (v + 1) * nocc] * occ


def hartree(coulomb, occ_own, densities):
    rows, nocc = occ_own.shape
    width = densities[0].shape[0] * nocc
    return pl.pallas_call(
        potential_kernel,
        out_shape=jax.ShapeDtypeStruct((rows, width), jnp.float32),
        compiler_params=pltpu.CompilerParams(vmem_limit_bytes=12 * MIB),
        cost_estimate=pl.CostEstimate(
            flops=2 * coulomb.size * width, bytes_accessed=2 * coulomb.size, transcendentals=0
        ),
    )(coulomb, occ_own, *densities)


def finish_kernel(direct_ref, z_ref, vir_ref, out_ref):
    coupling = (direct_ref[...] - z_ref[...].astype(jnp.float32)).astype(jnp.bfloat16)
    out_ref[...] = lax.dot_general(
        vir_ref[...], coupling, (((0,), (0,)), ((), ())), preferred_element_type=jnp.float32
    ).astype(jnp.bfloat16)


def finish(direct, z_own, vir_own):
    width = direct.shape[1]
    return pl.pallas_call(
        finish_kernel,
        out_shape=jax.ShapeDtypeStruct((vir_own.shape[1], width), jnp.bfloat16),
        compiler_params=pltpu.CompilerParams(vmem_limit_bytes=12 * MIB),
        cost_estimate=pl.CostEstimate(
            flops=2 * vir_own.size * width, bytes_accessed=2 * vir_own.size, transcendentals=0
        ),
    )(direct, z_own, vir_own)


def swap(x, axis, offset):
    return lax.ppermute(x, axis, [(i, i ^ offset) for i in range(lax.axis_size(axis))])


def over_chips(block):
    kpoints = lax.axis_size("ka")
    return [block] + [swap(block, "ka", s) for s in range(2, kpoints, 2)]


def trade(x, axis):
    return lax.all_to_all(x, axis, split_axis=0, concat_axis=0, tiled=True)


def per_device(
    occ_rows, vir_rows, trial_vectors, occ_energy, vir_energy, coulomb, exch_kernel, minus_table
):
    vectors, nocc, own_virtual = trial_vectors.shape[1:]
    own_rows = occ_rows.shape[1]
    kpoints = lax.axis_size("ka")
    bands = lax.axis_size("band")
    occ_own, vir_own = occ_rows[0], vir_rows[0]
    width = vectors * nocc
    copies = spread(jnp.swapaxes(trial_vectors[0], 1, 2), bands)
    trial_full = trade(copies, "band")
    trial_full = trial_full.reshape(bands * own_virtual, width)

    direct = [s for s in range(1, bands) if s & (s - 1) == 0]
    remote = [s for s in range(1, bands) if s & (s - 1)]
    parts = over_chips(occ_own)
    moved = {s: swap(occ_own, "band", s) for s in remote}

    y_own = prepare(kpoints, vir_own, trial_full, occ_own)
    y_all = trade(y_own, "ka")

    parts, y_own = lax.optimization_barrier((parts, y_own))
    near = {0: jnp.stack(parts)}
    near.update({s: swap(near[0], "band", s) for s in direct})
    near.update({s: jnp.stack(over_chips(moved[s])) for s in remote})

    density = summed_density(vectors, own_rows, y_all)
    densities = [density] + [swap(density, "band", s) for s in range(1, bands)]
    potential = hartree(coulomb, occ_own, densities)

    blocks = []
    for s in range(bands):
        blocks += [near[s], swap(near[s], "ka", 1)]
    z_all = exchange(minus_table, y_all, blocks, exch_kernel)

    z_own = trade(z_all, "ka")
    partial_sums = finish(potential, z_own.reshape(own_rows, width), vir_own)
    parts = trade(partial_sums.reshape(bands, own_virtual, width), "band")
    coupled = jnp.sum(parts.astype(jnp.float32), axis=0).reshape(own_virtual, vectors, nocc)
    coupled = jnp.transpose(coupled, (1, 2, 0))
    energy_gaps = vir_energy[0][None, :] - occ_energy[0][:, None]
    return (energy_gaps[None] * trial_vectors[0] + coupled)[None]


def solution(mesh):
    in_specs = (
        P("ka", "band", None),
        P("ka", "band", None),
        P("ka", None, None, "band"),
        P("ka", None),
        P("ka", "band"),
        P("band", None),
        P(None, "band", None),
        P(),
    )
    out_specs = P("ka", None, None, "band")

    return jax.shard_map(
        per_device, mesh=mesh, in_specs=in_specs, out_specs=out_specs, check_vma=False
    )
```

profile of v0, /device:TPU:0, one launch (start us, length us, event | category | flops | bytes accessed | tf_op | source)
XLA Modules:
  0.0 100.6 jit_solution(8583652162281847586)
XLA Ops:
  1.8 5.2 %all-to-all-start = ((bf16[4,224,256]{2,1,0:T(8,128)(2,1)}), bf16[4,224,256]{2,1,0:T(8,128)(2,1)S(1)}, u32[]{:S(2)}, u32[]{:S(2)}) async-start(bf16[4,224,256]{2,1,0:T(8,128)(2,1)} %shard_map.85), calls=%async_computation | async-start | bytes 917504 | tf_op jit(solution)/shard_map/all_to_all | solution.py:288
  7.0 1.6 %collective-permute-start.3 = (bf16[512,128]{1,0:T(8,128)(2,1)}, bf16[512,128]{1,0:T(8,128)(2,1)S(1)}, u32[]{:S(2)}, u32[]{:S(2)}) collective-permute-start(bf16[512,128]{1,0:T(8,128)(2,1)} %bitcast.41), channel_id=1, source_target_pairs={{0,8},{4,12},{8,0},{12,4},{16,24},{20,28},{24,16},{28,20},{1,9},{5... | collective-permute-start | bytes 393224 | tf_op jit(solution)/shard_map/ppermute | solution.py:279
  8.5 2.6 %collective-permute-start.4 = (bf16[512,128]{1,0:T(8,128)(2,1)}, bf16[512,128]{1,0:T(8,128)(2,1)S(1)}, u32[]{:S(2)}, u32[]{:S(2)}) collective-permute-start(bf16[512,128]{1,0:T(8,128)(2,1)} %bitcast.42), channel_id=1, source_target_pairs={{0,16},{4,20},{8,24},{12,28},{16,0},{20,4},{24,8},{28,12},{1,17},{... | collective-permute-start | bytes 393224 | tf_op jit(solution)/shard_map/ppermute | solution.py:279
  11.4 2.9 %all-to-all-done = bf16[4,224,256]{2,1,0:T(8,128)(2,1)S(1)} async-done(((bf16[4,224,256]{2,1,0:T(8,128)(2,1)}), bf16[4,224,256]{2,1,0:T(8,128)(2,1)S(1)}, u32[]{:S(2)}, u32[]{:S(2)}) %all-to-all-start) | async-done | bytes 458784 | tf_op jit(solution)/shard_map/all_to_all | solution.py:288
  16.4 1.8 %shard_map.86 = bf16[8,80,256]{2,1,0:T(8,128)(2,1)} custom-call(bf16[512,896]{1,0:T(8,128)(2,1)S(1)} %bitcast.38, bf16[896,256]{1,0:T(8,128)(2,1)S(1)} %bitcast.40, bf16[512,128]{1,0:T(8,128)(2,1)S(1)} %bitcast.44), custom_call_target="tpu_custom_call" | custom-call | flops 234881024 | bytes 917504 | tf_op jit(solution)/shard_map/pallas_call | solution.py:69
  18.2 3.3 %collective-permute-done.4 = bf16[512,128]{1,0:T(8,128)(2,1)S(1)} collective-permute-done((bf16[512,128]{1,0:T(8,128)(2,1)}, bf16[512,128]{1,0:T(8,128)(2,1)S(1)}, u32[]{:S(2)}, u32[]{:S(2)}) %collective-permute-start.4) | collective-permute-done | bytes 131104 | tf_op jit(solution)/shard_map/ppermute | solution.py:279
  22.4 1.6 %collective-permute-start.9 = (bf16[4,512,128]{2,1,0:T(8,128)(2,1)}, bf16[4,512,128]{2,1,0:T(8,128)(2,1)}, u32[]{:S(2)}, u32[]{:S(2)}) collective-permute-start(bf16[4,512,128]{2,1,0:T(8,128)(2,1)} %pad_maximum_fusion.refs_0_), channel_id=1, source_target_pairs={{0,2},{1,3},{2,0},{3,1},{4,6},{5,7},{6,4},{7,5},{8,10},{9,11},{10,... | collective-permute-start | bytes 1572872 | tf_op jit(solution)/shard_map/ppermute | solution.py:279
  24.0 1.5 %collective-permute-start.7 = (bf16[4,512,128]{2,1,0:T(8,128)(2,1)}, bf16[4,512,128]{2,1,0:T(8,128)(2,1)}, u32[]{:S(2)}, u32[]{:S(2)}) collective-permute-start(bf16[4,512,128]{2,1,0:T(8,128)(2,1)} %pad_maximum_fusion.refs_0_), channel_id=1, source_target_pairs={{0,1},{1,0},{2,3},{3,2},{4,5},{5,4},{6,7},{7,6},{8,9},{9,8},{10,11... | collective-permute-start | bytes 1572872 | tf_op jit(solution)/shard_map/ppermute | solution.py:279
  25.9 11.8 %collective-permute-done.11 = bf16[512,128]{1,0:T(8,128)(2,1)S(1)} collective-permute-done((bf16[512,128]{1,0:T(8,128)(2,1)S(1)}, bf16[512,128]{1,0:T(8,128)(2,1)S(1)}, u32[]{:S(2)}, u32[]{:S(2)}) %collective-permute-start.11) | collective-permute-done | bytes 131104 | tf_op jit(solution)/shard_map/ppermute | solution.py:279
  37.6 3.5 %collective-permute-start.12 = (bf16[512,128]{1,0:T(8,128)(2,1)S(1)}, bf16[512,128]{1,0:T(8,128)(2,1)S(1)}, u32[]{:S(2)}, u32[]{:S(2)}) collective-permute-start(bf16[512,128]{1,0:T(8,128)(2,1)S(1)} %collective-permute-done.11), channel_id=1, source_target_pairs={{0,8},{4,12},{8,0},{12,4},{16,24},{20,28},{24,16},{28,20},{1,9},{5... | collective-permute-start | bytes 393224 | tf_op jit(solution)/shard_map/ppermute | solution.py:279
  42.2 1.5 %collective-permute-start.14 = (bf16[512,128]{1,0:T(8,128)(2,1)S(1)}, bf16[512,128]{1,0:T(8,128)(2,1)S(1)}, u32[]{:S(2)}, u32[]{:S(2)}) collective-permute-start(bf16[512,128]{1,0:T(8,128)(2,1)S(1)} %collective-permute-done.11), channel_id=1, source_target_pairs={{0,24},{4,28},{8,16},{12,20},{16,8},{20,12},{24,0},{28,4},{1,25},{... | collective-permute-start | bytes 393224 | tf_op jit(solution)/shard_map/ppermute | solution.py:279
  43.7 3.6 %all-to-all-start.1 = ((bf16[8,80,256]{2,1,0:T(8,128)(2,1)}), bf16[8,80,256]{2,1,0:T(8,128)(2,1)S(1)}, u32[]{:S(2)}, u32[]{:S(2)}) async-start(bf16[8,80,256]{2,1,0:T(8,128)(2,1)} %shard_map.86), calls=%async_computation.1 | async-start | bytes 655360 | tf_op jit(solution)/shard_map/all_to_all | solution.py:288
  47.3 4.4 %collective-permute-done.13 = bf16[512,128]{1,0:T(8,128)(2,1)S(1)} collective-permute-done((bf16[512,128]{1,0:T(8,128)(2,1)S(1)}, bf16[512,128]{1,0:T(8,128)(2,1)S(1)}, u32[]{:S(2)}, u32[]{:S(2)}) %collective-permute-start.13) | collective-permute-done | bytes 131104 | tf_op jit(solution)/shard_map/ppermute | solution.py:279
  54.7 5.3 %all-to-all-done.1.y_ref = bf16[8,80,256]{2,1,0:T(8,128)(2,1)S(1)} async-done(((bf16[8,80,256]{2,1,0:T(8,128)(2,1)}), bf16[8,80,256]{2,1,0:T(8,128)(2,1)S(1)}, u32[]{:S(2)}, u32[]{:S(2)}) %all-to-all-start.1) | async-done | bytes 327712 | tf_op jit(solution)/shard_map/all_to_all | solution.py:288
  60.7 11.3 %shard_map.89 = bf16[8,64,256]{2,1,0:T(8,128)(2,1)} custom-call(bf16[8,80,256]{2,1,0:T(8,128)(2,1)} %copy-done.3, s32[8,8]{1,0:T(8,128)} %table_hbm.1, bf16[8,512,2048]{2,1,0:T(8,128)(2,1)} %exch_hbm.1, bf16[4,512,128]{2,1,0:T(8,128)(2,1)} %pad_maximum_fusion.refs_0_, bf16[4,512,128]{2,1,0:T(8,128)(2,1)} %collective-permute-done.6.refs_1_, ...), custom_call_target="tpu_custom_call" | custom-call | flops 17179869184 | bytes 6291456 | tf_op jit(solution)/shard_map/pallas_call | solution.py:172
  71.9 4.3 %all-to-all-start.2 = ((bf16[8,64,256]{2,1,0:T(8,128)(2,1)}), bf16[8,64,256]{2,1,0:T(8,128)(2,1)}, u32[]{:S(2)}, u32[]{:S(2)}) async-start(bf16[8,64,256]{2,1,0:T(8,128)(2,1)} %shard_map.89), calls=%async_computation.2 | async-start | bytes 524288 | tf_op jit(solution)/shard_map/all_to_all | solution.py:288
  77.2 1.4 %collective-permute-start = (bf16[2,512]{1,0:T(2,128)(2,1)S(1)}, bf16[2,512]{1,0:T(2,128)(2,1)S(1)}, u32[]{:S(2)}, u32[]{:S(2)}) collective-permute-start(bf16[2,512]{1,0:T(2,128)(2,1)S(1)} %shard_map.87.refs_0_), channel_id=1, source_target_pairs={{0,1},{1,0},{2,3},{3,2},{4,5},{5,4},{6,7},{7,6},{8,9},{9,8},{10,11... | collective-permute-start | bytes 6152 | tf_op jit(solution)/shard_map/ppermute | solution.py:279
  78.7 1.5 %collective-permute-start.1 = (bf16[2,512]{1,0:T(2,128)(2,1)S(1)}, bf16[2,512]{1,0:T(2,128)(2,1)S(1)}, u32[]{:S(2)}, u32[]{:S(2)}) collective-permute-start(bf16[2,512]{1,0:T(2,128)(2,1)S(1)} %shard_map.87.refs_0_), channel_id=1, source_target_pairs={{0,2},{1,3},{2,0},{3,1},{4,6},{5,7},{6,4},{7,5},{8,10},{9,11},{10,... | collective-permute-start | bytes 6152 | tf_op jit(solution)/shard_map/ppermute | solution.py:279
  80.9 1.4 %collective-permute-done.1.refs_2_ = bf16[2,512]{1,0:T(2,128)(2,1)S(1)} collective-permute-done((bf16[2,512]{1,0:T(2,128)(2,1)S(1)}, bf16[2,512]{1,0:T(2,128)(2,1)S(1)}, u32[]{:S(2)}, u32[]{:S(2)}) %collective-permute-start.1) | collective-permute-done | bytes 2080 | tf_op jit(solution)/shard_map/ppermute | solution.py:279
  82.3 2.4 %collective-permute-done.2.refs_3_ = bf16[2,512]{1,0:T(2,128)(2,1)S(1)} collective-permute-done((bf16[2,512]{1,0:T(2,128)(2,1)S(1)}, bf16[2,512]{1,0:T(2,128)(2,1)S(1)}, u32[]{:S(2)}, u32[]{:S(2)}) %collective-permute-start.2) | collective-permute-done | bytes 2080 | tf_op jit(solution)/shard_map/ppermute | solution.py:279
  86.3 2.2 %shard_map.90 = bf16[896,256]{1,0:T(8,128)(2,1)} custom-call(f32[512,256]{1,0:T(8,128)S(1)} %shard_map.88.direct_ref, bf16[512,256]{1,0:T(8,128)(2,1)} %bitcast.15.z_ref, bf16[512,896]{1,0:T(8,128)(2,1)S(1)} %bitcast.39), custom_call_target="tpu_custom_call" | custom-call | flops 234881024 | bytes 917504 | tf_op jit(solution)/shard_map/pallas_call | solution.py:268
  88.5 3.5 %all-to-all-start.3 = ((bf16[4,224,256]{2,1,0:T(8,128)(2,1)}), bf16[4,224,256]{2,1,0:T(8,128)(2,1)S(1)}, u32[]{:S(2)}, u32[]{:S(2)}) async-start(bf16[4,224,256]{2,1,0:T(8,128)(2,1)} %bitcast.16), calls=%async_computation.3 | async-start | bytes 917504 | tf_op jit(solution)/shard_map/all_to_all | solution.py:288
  92.1 6.8 %all-to-all-done.3 = bf16[4,224,256]{2,1,0:T(8,128)(2,1)S(1)} async-done(((bf16[4,224,256]{2,1,0:T(8,128)(2,1)}), bf16[4,224,256]{2,1,0:T(8,128)(2,1)S(1)}, u32[]{:S(2)}, u32[]{:S(2)}) %all-to-all-start.3) | async-done | bytes 458784 | tf_op jit(solution)/shard_map/all_to_all | solution.py:288
  98.9 1.7 %fusion.1 = f32[1,2,128,224]{2,3,1,0:T(8,128)} fusion(f32[1,2,128,224]{2,3,1,0:T(8,128)} %param.10, f32[128,224]{0,1:T(8,128)S(1)} %broadcast_subtract_fusion, f32[224,256]{1,0:T(8,128)S(1)} %convert_reduce_fusion), kind=kLoop, calls=%fused_computation.5 | loop fusion | flops 114688 | bytes 802816 | tf_op jit(solution)/shard_map/broadcast_in_dim | solution.py:332
  (51 shorter events, 13.7 us)
Async XLA Ops:
  1.8 12.5 %all-to-all-start = ((bf16[4,224,256]{2,1,0:T(8,128)(2,1)}), bf16[4,224,256]{2,1,0:T(8,128)(2,1)S(1)}, u32[]{:S(2)}, u32[]{:S(2)}) async-start(bf16[4,224,256]{2,1,0:T(8,128)(2,1)} %shard_map.85), calls=%async_computation | async-start | bytes 917504 | tf_op jit(solution)/shard_map/all_to_all | solution.py:288
  7.0 11.3 %collective-permute-start.3 = (bf16[512,128]{1,0:T(8,128)(2,1)}, bf16[512,128]{1,0:T(8,128)(2,1)S(1)}, u32[]{:S(2)}, u32[]{:S(2)}) collective-permute-start(bf16[512,128]{1,0:T(8,128)(2,1)} %bitcast.41), channel_id=1, source_target_pairs={{0,8},{4,12},{8,0},{12,4},{16,24},{20,28},{24,16},{28,20},{1,9},{5... | collective-permute-start | bytes 393224 | tf_op jit(solution)/shard_map/ppermute | solution.py:279
  8.5 13.0 %collective-permute-start.4 = (bf16[512,128]{1,0:T(8,128)(2,1)}, bf16[512,128]{1,0:T(8,128)(2,1)S(1)}, u32[]{:S(2)}, u32[]{:S(2)}) collective-permute-start(bf16[512,128]{1,0:T(8,128)(2,1)} %bitcast.42), channel_id=1, source_target_pairs={{0,16},{4,20},{8,24},{12,28},{16,0},{20,4},{24,8},{28,12},{1,17},{... | collective-permute-start | bytes 393224 | tf_op jit(solution)/shard_map/ppermute | solution.py:279
  11.1 10.4 %collective-permute-start.5 = (bf16[512,128]{1,0:T(8,128)(2,1)}, bf16[512,128]{1,0:T(8,128)(2,1)S(1)}, u32[]{:S(2)}, u32[]{:S(2)}) collective-permute-start(bf16[512,128]{1,0:T(8,128)(2,1)} %bitcast.43), channel_id=1, source_target_pairs={{0,24},{4,28},{8,16},{12,20},{16,8},{20,12},{24,0},{28,4},{1,25},{... | collective-permute-start | bytes 393224 | tf_op jit(solution)/shard_map/ppermute | solution.py:279
  22.4 30.0 %collective-permute-start.9 = (bf16[4,512,128]{2,1,0:T(8,128)(2,1)}, bf16[4,512,128]{2,1,0:T(8,128)(2,1)}, u32[]{:S(2)}, u32[]{:S(2)}) collective-permute-start(bf16[4,512,128]{2,1,0:T(8,128)(2,1)} %pad_maximum_fusion.refs_0_), channel_id=1, source_target_pairs={{0,2},{1,3},{2,0},{3,1},{4,6},{5,7},{6,4},{7,5},{8,10},{9,11},{10,... | collective-permute-start | bytes 1572872 | tf_op jit(solution)/shard_map/ppermute | solution.py:279
  24.0 28.5 %collective-permute-start.7 = (bf16[4,512,128]{2,1,0:T(8,128)(2,1)}, bf16[4,512,128]{2,1,0:T(8,128)(2,1)}, u32[]{:S(2)}, u32[]{:S(2)}) collective-permute-start(bf16[4,512,128]{2,1,0:T(8,128)(2,1)} %pad_maximum_fusion.refs_0_), channel_id=1, source_target_pairs={{0,1},{1,0},{2,3},{3,2},{4,5},{5,4},{6,7},{7,6},{8,9},{9,8},{10,11... | collective-permute-start | bytes 1572872 | tf_op jit(solution)/shard_map/ppermute | solution.py:279
  25.5 12.1 %collective-permute-start.11 = (bf16[512,128]{1,0:T(8,128)(2,1)S(1)}, bf16[512,128]{1,0:T(8,128)(2,1)S(1)}, u32[]{:S(2)}, u32[]{:S(2)}) collective-permute-start(bf16[512,128]{1,0:T(8,128)(2,1)S(1)} %bitcast.45), channel_id=1, source_target_pairs={{0,3},{1,2},{2,1},{3,0},{4,7},{5,6},{6,5},{7,4},{8,11},{9,10},{10,... | collective-permute-start | bytes 393224 | tf_op jit(solution)/shard_map/ppermute | solution.py:279
  37.6 9.7 %collective-permute-start.12 = (bf16[512,128]{1,0:T(8,128)(2,1)S(1)}, bf16[512,128]{1,0:T(8,128)(2,1)S(1)}, u32[]{:S(2)}, u32[]{:S(2)}) collective-permute-start(bf16[512,128]{1,0:T(8,128)(2,1)S(1)} %collective-permute-done.11), channel_id=1, source_target_pairs={{0,8},{4,12},{8,0},{12,4},{16,24},{20,28},{24,16},{28,20},{1,9},{5... | collective-permute-start | bytes 393224 | tf_op jit(solution)/shard_map/ppermute | solution.py:279
  41.1 10.6 %collective-permute-start.13 = (bf16[512,128]{1,0:T(8,128)(2,1)S(1)}, bf16[512,128]{1,0:T(8,128)(2,1)S(1)}, u32[]{:S(2)}, u32[]{:S(2)}) collective-permute-start(bf16[512,128]{1,0:T(8,128)(2,1)S(1)} %collective-permute-done.11), channel_id=1, source_target_pairs={{0,16},{4,20},{8,24},{12,28},{16,0},{20,4},{24,8},{28,12},{1,17},{... | collective-permute-start | bytes 393224 | tf_op jit(solution)/shard_map/ppermute | solution.py:279
  42.2 9.5 %collective-permute-start.14 = (bf16[512,128]{1,0:T(8,128)(2,1)S(1)}, bf16[512,128]{1,0:T(8,128)(2,1)S(1)}, u32[]{:S(2)}, u32[]{:S(2)}) collective-permute-start(bf16[512,128]{1,0:T(8,128)(2,1)S(1)} %collective-permute-done.11), channel_id=1, source_target_pairs={{0,24},{4,28},{8,16},{12,20},{16,8},{20,12},{24,0},{28,4},{1,25},{... | collective-permute-start | bytes 393224 | tf_op jit(solution)/shard_map/ppermute | solution.py:279
  43.7 16.2 %all-to-all-start.1 = ((bf16[8,80,256]{2,1,0:T(8,128)(2,1)}), bf16[8,80,256]{2,1,0:T(8,128)(2,1)S(1)}, u32[]{:S(2)}, u32[]{:S(2)}) async-start(bf16[8,80,256]{2,1,0:T(8,128)(2,1)} %shard_map.86), calls=%async_computation.1 | async-start | bytes 655360 | tf_op jit(solution)/shard_map/all_to_all | solution.py:288
  51.8 32.9 %copy-start.2 = (bf16[512,2048]{1,0:T(8,128)(2,1)S(1)}, bf16[512,2048]{1,0:T(8,128)(2,1)}, u32[]{:S(2)}) copy-start(bf16[512,2048]{1,0:T(8,128)(2,1)} %coulomb_ref.1) | copy-start | bytes 6291460
  51.8 34.5 %copy-start.1 = (bf16[1,512,896]{2,1,0:T(8,128)(2,1)S(1)}, bf16[1,512,896]{2,1,0:T(8,128)(2,1)}, u32[]{:S(2)}) copy-start(bf16[1,512,896]{2,1,0:T(8,128)(2,1)} %param.9) | copy-start | bytes 2752516
  51.8 40.2 %copy-start.9 = (f32[1,224]{1,0:T(1,128)S(1)}, f32[1,224]{1,0:T(1,128)}, u32[]{:S(2)}) copy-start(f32[1,224]{1,0:T(1,128)} %param.12) | copy-start | bytes 2692
  51.8 40.2 %copy-start.10 = (f32[1,128]{1,0:T(1,128)S(1)}, f32[1,128]{1,0:T(1,128)}, u32[]{:S(2)}) copy-start(f32[1,128]{1,0:T(1,128)} %param.11) | copy-start | bytes 1540
  51.8 2.0 %collective-permute-start.15 = (bf16[4,512,128]{2,1,0:T(8,128)(2,1)S(1)}, bf16[4,512,128]{2,1,0:T(8,128)(2,1)S(1)}, u32[]{:S(2)}, u32[]{:S(2)}) collective-permute-start(bf16[4,512,128]{2,1,0:T(8,128)(2,1)S(1)} %pad_maximum_fusion.1.refs_6_), channel_id=1, source_target_pairs={{0,4},{4,0},{8,12},{12,8},{16,20},{20,16},{24,28},{28,24},{1,5},{5... | collective-permute-start | bytes 1572872 | tf_op jit(solution)/shard_map/ppermute | solution.py:279
  51.9 2.8 %collective-permute-start.6 = (bf16[4,512,128]{2,1,0:T(8,128)(2,1)}, bf16[4,512,128]{2,1,0:T(8,128)(2,1)}, u32[]{:S(2)}, u32[]{:S(2)}) collective-permute-start(bf16[4,512,128]{2,1,0:T(8,128)(2,1)} %pad_maximum_fusion.refs_0_), channel_id=1, source_target_pairs={{0,4},{4,0},{8,12},{12,8},{16,20},{20,16},{24,28},{28,24},{1,5},{5... | collective-permute-start | bytes 1572872 | tf_op jit(solution)/shard_map/ppermute | solution.py:279
  52.4 7.5 %collective-permute-start.10 = (bf16[4,512,128]{2,1,0:T(8,128)(2,1)}, bf16[4,512,128]{2,1,0:T(8,128)(2,1)}, u32[]{:S(2)}, u32[]{:S(2)}) collective-permute-start(bf16[4,512,128]{2,1,0:T(8,128)(2,1)} %collective-permute-done.9.refs_4_), channel_id=1, source_target_pairs={{0,4},{4,0},{8,12},{12,8},{16,20},{20,16},{24,28},{28,24},{1,5},{5... | collective-permute-start | bytes 1572872 | tf_op jit(solution)/shard_map/ppermute | solution.py:279
  52.5 7.5 %collective-permute-start.8 = (bf16[4,512,128]{2,1,0:T(8,128)(2,1)}, bf16[4,512,128]{2,1,0:T(8,128)(2,1)}, u32[]{:S(2)}, u32[]{:S(2)}) collective-permute-start(bf16[4,512,128]{2,1,0:T(8,128)(2,1)} %collective-permute-done.7.refs_2_), channel_id=1, source_target_pairs={{0,4},{4,0},{8,12},{12,8},{16,20},{20,16},{24,28},{28,24},{1,5},{5... | collective-permute-start | bytes 1572872 | tf_op jit(solution)/shard_map/ppermute | solution.py:279
  71.9 14.3 %all-to-all-start.2 = ((bf16[8,64,256]{2,1,0:T(8,128)(2,1)}), bf16[8,64,256]{2,1,0:T(8,128)(2,1)}, u32[]{:S(2)}, u32[]{:S(2)}) async-start(bf16[8,64,256]{2,1,0:T(8,128)(2,1)} %shard_map.89), calls=%async_computation.2 | async-start | bytes 524288 | tf_op jit(solution)/shard_map/all_to_all | solution.py:288
  77.2 3.7 %collective-permute-start = (bf16[2,512]{1,0:T(2,128)(2,1)S(1)}, bf16[2,512]{1,0:T(2,128)(2,1)S(1)}, u32[]{:S(2)}, u32[]{:S(2)}) collective-permute-start(bf16[2,512]{1,0:T(2,128)(2,1)S(1)} %shard_map.87.refs_0_), channel_id=1, source_target_pairs={{0,1},{1,0},{2,3},{3,2},{4,5},{5,4},{6,7},{7,6},{8,9},{9,8},{10,11... | collective-permute-start | bytes 6152 | tf_op jit(solution)/shard_map/ppermute | solution.py:279
  78.7 3.6 %collective-permute-start.1 = (bf16[2,512]{1,0:T(2,128)(2,1)S(1)}, bf16[2,512]{1,0:T(2,128)(2,1)S(1)}, u32[]{:S(2)}, u32[]{:S(2)}) collective-permute-start(bf16[2,512]{1,0:T(2,128)(2,1)S(1)} %shard_map.87.refs_0_), channel_id=1, source_target_pairs={{0,2},{1,3},{2,0},{3,1},{4,6},{5,7},{6,4},{7,5},{8,10},{9,11},{10,... | collective-permute-start | bytes 6152 | tf_op jit(solution)/shard_map/ppermute | solution.py:279
  80.1 4.5 %collective-permute-start.2 = (bf16[2,512]{1,0:T(2,128)(2,1)S(1)}, bf16[2,512]{1,0:T(2,128)(2,1)S(1)}, u32[]{:S(2)}, u32[]{:S(2)}) collective-permute-start(bf16[2,512]{1,0:T(2,128)(2,1)S(1)} %shard_map.87.refs_0_), channel_id=1, source_target_pairs={{0,3},{1,2},{2,1},{3,0},{4,7},{5,6},{6,5},{7,4},{8,11},{9,10},{10,... | collective-permute-start | bytes 6152 | tf_op jit(solution)/shard_map/ppermute | solution.py:279
  88.5 10.4 %all-to-all-start.3 = ((bf16[4,224,256]{2,1,0:T(8,128)(2,1)}), bf16[4,224,256]{2,1,0:T(8,128)(2,1)S(1)}, u32[]{:S(2)}, u32[]{:S(2)}) async-start(bf16[4,224,256]{2,1,0:T(8,128)(2,1)} %bitcast.16), calls=%async_computation.3 | async-start | bytes 917504 | tf_op jit(solution)/shard_map/all_to_all | solution.py:288
  (8 other events, 8.5 us)
where the time goes:
time: 101 us
  waiting for transfers between devices  39.2 us (39%)
  starting transfers between devices  35.2 us (35%)
  Pallas kernels  16.9 us (17%)
  local copies, waits for them, and re-layouts  6.45 us (6%)
  other arithmetic  2.75 us (3%)
    ppermute x16, waiting for transfers between devices, swap(): lax.ppermute(x, axis, [(i, i ^ offset) for i in range(lax.axis_size(axis))])  24.2 us
    ppermute x16, starting transfers between devices, swap(): lax.ppermute(x, axis, [(i, i ^ offset) for i in range(lax.axis_size(axis))])  18.6 us
    all_to_all x4, starting transfers between devices, trade(): return lax.all_to_all(x, axis, split_axis=0, concat_axis=0, tiled=True)  16.6 us
    all_to_all x4, waiting for transfers between devices, trade(): return lax.all_to_all(x, axis, split_axis=0, concat_axis=0, tiled=True)  15 us
    pallas_call x1, Pallas kernels, exchange(): pl.pallas_call(exchange_kernel, in_specs=[held] + [pl.BlockSpec(memory_sp...  11.3 us
    unnamed x24, local copies, waits for them, and re-layouts  6.45 us
    pallas_call x1, Pallas kernels, finish(): pl.pallas_call(finish_kernel, out_shape=jax.ShapeDtypeStruct((vir_own.sha...  2.17 us
  transfers between devices with their start and end apart: 20, of which 11 were waited for; matrix products, arithmetic and copies ran while one was open for 0% of the time, Pallas kernels for 3%

commit v1 on v0

--- a/solution.py
+++ b/solution.py
@@ -11,27 +11,29 @@
 EXTRA = 16
 
 
-def spread_kernel(trial_ref, out_ref):
-    copies = out_ref.shape[0]
+def round_kernel(trial_ref, out_ref):
     vectors, _, nocc = trial_ref.shape
     for v in range(vectors):
-        rounded = trial_ref[v].astype(jnp.bfloat16)
-        for b in range(copies):
-            out_ref[b, :, v * nocc : (v + 1) * nocc] = rounded
-
-
-def spread(trial, copies):
+        out_ref[:, v * nocc : (v + 1) * nocc] = trial_ref[v].astype(jnp.bfloat16)
+
+
+def rounded(trial):
     vectors, virtual, nocc = trial.shape
     return pl.pallas_call(
-        spread_kernel,
-        out_shape=jax.ShapeDtypeStruct((copies, virtual, vectors * nocc), jnp.bfloat16),
+        round_kernel,
+        out_shape=jax.ShapeDtypeStruct((virtual, vectors * nocc), jnp.bfloat16),
         compiler_params=pltpu.CompilerParams(vmem_limit_bytes=12 * MIB),
     )(trial)
 
 
-def prepare_kernel(vir_ref, trial_ref, occ_hbm, out_ref, occ_ref, arrived):
+def prepare_kernel(vir_ref, occ_hbm, *refs):
+    parts, (out_ref, trial_ref, occ_ref, arrived) = refs[:-4], refs[-4:]
     copy = pltpu.make_async_copy(occ_hbm, occ_ref, arrived)
     copy.start()
+    band = lax.axis_index("band").astype(jnp.int32)
+    virtual = parts[0].shape[0]
+    for s, part in enumerate(parts):
+        trial_ref[pl.ds(pl.multiple_of((band ^ s) * virtual, 16), virtual)] = part[...]
     kpoints, _, width = out_ref.shape
     rows, nocc = occ_ref.shape
     points = rows // kpoints
@@ -63,21 +65,25 @@
         out_ref[j, points:] = extra
 
 
-def prepare(kpoints, vir_own, trial_full, occ_own):
+def prepare(kpoints, vir_own, parts, occ_own):
     rows = occ_own.shape[0]
-    width = trial_full.shape[1]
+    width = parts[0].shape[1]
+    held = pl.BlockSpec(memory_space=pltpu.VMEM)
     return pl.pallas_call(
         prepare_kernel,
-        in_specs=[pl.BlockSpec(memory_space=pltpu.VMEM)] * 2
-        + [pl.BlockSpec(memory_space=pl.ANY)],
-        out_specs=pl.BlockSpec(memory_space=pltpu.VMEM),
-        scratch_shapes=[pltpu.VMEM(occ_own.shape, jnp.bfloat16), pltpu.SemaphoreType.DMA],
+        in_specs=[held, pl.BlockSpec(memory_space=pl.ANY)] + [held] * len(parts),
+        out_specs=held,
+        scratch_shapes=[
+            pltpu.VMEM((vir_own.shape[1], width), jnp.bfloat16),
+            pltpu.VMEM(occ_own.shape, jnp.bfloat16),
+            pltpu.SemaphoreType.DMA,
+        ],
         out_shape=jax.ShapeDtypeStruct((kpoints, rows // kpoints + EXTRA, width), jnp.bfloat16),
         compiler_params=pltpu.CompilerParams(vmem_limit_bytes=12 * MIB),
         cost_estimate=pl.CostEstimate(
             flops=2 * vir_own.size * width, bytes_accessed=2 * vir_own.size, transcendentals=0
         ),
-    )(vir_own, trial_full, occ_own)
+    )(vir_own, occ_own, *parts)
 
 
 def exchange_kernel(y_ref, table_hbm, exch_hbm, *refs):
@@ -256,18 +262,29 @@
     )(coulomb, occ_own, *densities)
 
 
-def finish_kernel(direct_ref, z_ref, vir_ref, out_ref):
+def finish_kernel(direct_ref, z_ref, vir_ref, *refs):
+    own_ref, sent_refs, total_ref = refs[0], refs[1:-1], refs[-1]
+    rows = own_ref.shape[0]
+    band = lax.axis_index("band").astype(jnp.int32)
     coupling = (direct_ref[...] - z_ref[...].astype(jnp.float32)).astype(jnp.bfloat16)
-    out_ref[...] = lax.dot_general(
+    total_ref[...] = lax.dot_general(
         vir_ref[...], coupling, (((0,), (0,)), ((), ())), preferred_element_type=jnp.float32
-    ).astype(jnp.bfloat16)
-
-
-def finish(direct, z_own, vir_own):
+    )
+    own_ref[...] = total_ref[pl.ds(pl.multiple_of(band * rows, 8), rows)]
+    for s, sent_ref in enumerate(sent_refs):
+        first = pl.multiple_of((band ^ (s + 1)) * rows, 8)
+        sent_ref[...] = total_ref[pl.ds(first, rows)].astype(jnp.bfloat16)
+
+
+def finish(direct, z_own, vir_own, bands):
     width = direct.shape[1]
+    virtual = vir_own.shape[1]
+    part = (virtual // bands, width)
     return pl.pallas_call(
         finish_kernel,
-        out_shape=jax.ShapeDtypeStruct((vir_own.shape[1], width), jnp.bfloat16),
+        out_shape=[jax.ShapeDtypeStruct(part, jnp.float32)]
+        + [jax.ShapeDtypeStruct(part, jnp.bfloat16)] * (bands - 1),
+        scratch_shapes=[pltpu.VMEM((virtual, width), jnp.float32)],
         compiler_params=pltpu.CompilerParams(vmem_limit_bytes=12 * MIB),
         cost_estimate=pl.CostEstimate(
             flops=2 * vir_own.size * width, bytes_accessed=2 * vir_own.size, transcendentals=0
@@ -275,6 +292,25 @@
     )(direct, z_own, vir_own)
 
 
+def total_kernel(gap_ref, trial_ref, own_ref, *refs):
+    received, out_ref = refs[:-1], refs[-1]
+    vectors, _, nocc = out_ref.shape
+    for v in range(vectors):
+        part = slice(v * nocc, (v + 1) * nocc)
+        coupled = own_ref[:, part]
+        for ref in received:
+            coupled += ref[:, part].astype(jnp.float32)
+        out_ref[v] = gap_ref[...] * trial_ref[v] + coupled
+
+
+def total(gaps, trial, own, received):
+    return pl.pallas_call(
+        total_kernel,
+        out_shape=jax.ShapeDtypeStruct(trial.shape, jnp.float32),
+        compiler_params=pltpu.CompilerParams(vmem_limit_bytes=12 * MIB),
+    )(gaps, trial, own, *received)
+
+
 def swap(x, axis, offset):
     return lax.ppermute(x, axis, [(i, i ^ offset) for i in range(lax.axis_size(axis))])
 
@@ -291,22 +327,21 @@
 def per_device(
     occ_rows, vir_rows, trial_vectors, occ_energy, vir_energy, coulomb, exch_kernel, minus_table
 ):
-    vectors, nocc, own_virtual = trial_vectors.shape[1:]
+    vectors, nocc, _ = trial_vectors.shape[1:]
     own_rows = occ_rows.shape[1]
     kpoints = lax.axis_size("ka")
     bands = lax.axis_size("band")
     occ_own, vir_own = occ_rows[0], vir_rows[0]
     width = vectors * nocc
-    copies = spread(jnp.swapaxes(trial_vectors[0], 1, 2), bands)
-    trial_full = trade(copies, "band")
-    trial_full = trial_full.reshape(bands * own_virtual, width)
+    trial_own = rounded(jnp.swapaxes(trial_vectors[0], 1, 2))
+    trials = [trial_own] + [swap(trial_own, "band", s) for s in range(1, bands)]
 
     direct = [s for s in range(1, bands) if s & (s - 1) == 0]
     remote = [s for s in range(1, bands) if s & (s - 1)]
     parts = over_chips(occ_own)
     moved = {s: swap(occ_own, "band", s) for s in remote}
 
-    y_own = prepare(kpoints, vir_own, trial_full, occ_own)
+    y_own = prepare(kpoints, vir_own, trials, occ_own)
     y_all = trade(y_own, "ka")
 
     parts, y_own = lax.optimization_barrier((parts, y_own))
@@ -324,12 +359,11 @@
     z_all = exchange(minus_table, y_all, blocks, exch_kernel)
 
     z_own = trade(z_all, "ka")
-    partial_sums = finish(potential, z_own.reshape(own_rows, width), vir_own)
-    parts = trade(partial_sums.reshape(bands, own_virtual, width), "band")
-    coupled = jnp.sum(parts.astype(jnp.float32), axis=0).reshape(own_virtual, vectors, nocc)
-    coupled = jnp.transpose(coupled, (1, 2, 0))
-    energy_gaps = vir_energy[0][None, :] - occ_energy[0][:, None]
-    return (energy_gaps[None] * trial_vectors[0] + coupled)[None]
+    own, *sent = finish(potential, z_own.reshape(own_rows, width), vir_own, bands)
+    received = [swap(part, "band", s + 1) for s, part in enumerate(sent)]
+    gaps = vir_energy[0][:, None] - occ_energy[0][None, :]
+    sigma = total(gaps, jnp.swapaxes(trial_vectors[0], 1, 2), own, received)
+    return jnp.swapaxes(sigma, 1, 2)[None]
 
 
 def solution(mesh):

time: 101 us -> 96.3 us (0.953)
  waiting for transfers between devices: 39.2 us -> 35 us
    ppermute x16 -> x22, starting transfers between devices: 18.6 us -> 28.6 us  [swap(): lax.ppermute(x, axis, [(i, i ^ offset) for i in range(lax.axis_size(axis))])]
    all_to_all x4 -> x2, starting transfers between devices: 16.6 us -> 7.49 us  [trade(): return lax.all_to_all(x, axis, split_axis=0, concat_axis=0, tiled=True)]
    all_to_all x4 -> x2, waiting for transfers between devices: 15 us -> 7.86 us  [trade(): return lax.all_to_all(x, axis, split_axis=0, concat_axis=0, tiled=True)]
    ppermute x16 -> x22, waiting for transfers between devices: 24.2 us -> 27.2 us  [swap(): lax.ppermute(x, axis, [(i, i ^ offset) for i in range(lax.axis_size(axis))])]
    broadcast_in_dim x1 -> x0, other arithmetic: 1.67 us -> none  [per_device(): return (energy_gaps[None] * trial_vectors[0] + coupled)[None]]
    pallas_call x3 -> x4, Pallas kernels: 4.85 us -> 4.13 us  [the longest x1 1.9 us: prepare(): pl.pallas_call(prepare_kernel, in_specs=[held, pl.BlockSpec(memory_space=...]
    unnamed x24 -> x22, local copies, waits for them, and re-layouts: 6.45 us -> 6.56 us
  transfers between devices with their start and end apart: 20 -> 24, of which waited for: 11 -> 11; matrix products, arithmetic and copies ran while one was open for 0% -> 1% of each run, Pallas kernels for 3% -> 3%
where the time goes in v1:
time: 96.3 us; the launch traced here: 95.8 us
  starting transfers between devices  36.1 us (37%)
  waiting for transfers between devices  35 us (36%)
  Pallas kernels  16.1 us (17%)
  local copies, waits for them, and re-layouts  6.56 us (7%)
  other arithmetic  1.82 us (2%)
    ppermute x22, starting transfers between devices, swap(): lax.ppermute(x, axis, [(i, i ^ offset) for i in range(lax.axis_size(axis))])  28.6 us
    ppermute x22, waiting for transfers between devices, swap(): lax.ppermute(x, axis, [(i, i ^ offset) for i in range(lax.axis_size(axis))])  27.2 us
    pallas_call x1, Pallas kernels, exchange(): pl.pallas_call(exchange_kernel, in_specs=[held] + [pl.BlockSpec(memory_sp...  11.2 us
    all_to_all x2, waiting for transfers between devices, trade(): return lax.all_to_all(x, axis, split_axis=0, concat_axis=0, tiled=True)  7.86 us
    all_to_all x2, starting transfers between devices, trade(): return lax.all_to_all(x, axis, split_axis=0, concat_axis=0, tiled=True)  7.49 us
    unnamed x22, local copies, waits for them, and re-layouts  6.56 us
  transfers between devices with their start and end apart: 24, of which 11 were waited for; matrix products, arithmetic and copies ran while one was open for 1% of the time, Pallas kernels for 3%

profile of v1, /device:TPU:0, one launch (start us, length us, event | category | flops | bytes accessed | tf_op | source)
XLA Modules:
  0.0 95.8 jit_solution(3509954119354444820)
XLA Ops:
  1.0 3.0 %collective-permute-start = (bf16[224,256]{1,0:T(8,128)(2,1)S(1)}, bf16[224,256]{1,0:T(8,128)(2,1)S(1)}, u32[]{:S(2)}, u32[]{:S(2)}) collective-permute-start(bf16[224,256]{1,0:T(8,128)(2,1)S(1)} %shard_map.82.refs_0_), channel_id=1, source_target_pairs={{0,1},{1,0},{2,3},{3,2},{4,5},{5,4},{6,7},{7,6},{8,9},{9,8},{10,11... | collective-permute-start | bytes 344072 | tf_op jit(solution)/shard_map/ppermute | solution.py:315
  4.0 1.5 %collective-permute-start.1 = (bf16[224,256]{1,0:T(8,128)(2,1)S(1)}, bf16[224,256]{1,0:T(8,128)(2,1)S(1)}, u32[]{:S(2)}, u32[]{:S(2)}) collective-permute-start(bf16[224,256]{1,0:T(8,128)(2,1)S(1)} %shard_map.82.refs_0_), channel_id=1, source_target_pairs={{0,2},{1,3},{2,0},{3,1},{4,6},{5,7},{6,4},{7,5},{8,10},{9,11},{10,... | collective-permute-start | bytes 344072 | tf_op jit(solution)/shard_map/ppermute | solution.py:315
  5.5 2.0 %collective-permute-start.6 = (bf16[512,128]{1,0:T(8,128)(2,1)}, bf16[512,128]{1,0:T(8,128)(2,1)S(1)}, u32[]{:S(2)}, u32[]{:S(2)}) collective-permute-start(bf16[512,128]{1,0:T(8,128)(2,1)} %bitcast.21), channel_id=1, source_target_pairs={{0,8},{4,12},{8,0},{12,4},{16,24},{20,28},{24,16},{28,20},{1,9},{5... | collective-permute-start | bytes 393224 | tf_op jit(solution)/shard_map/ppermute | solution.py:315
  7.6 2.6 %collective-permute-start.7 = (bf16[512,128]{1,0:T(8,128)(2,1)}, bf16[512,128]{1,0:T(8,128)(2,1)S(1)}, u32[]{:S(2)}, u32[]{:S(2)}) collective-permute-start(bf16[512,128]{1,0:T(8,128)(2,1)} %bitcast.22), channel_id=1, source_target_pairs={{0,16},{4,20},{8,24},{12,28},{16,0},{20,4},{24,8},{28,12},{1,17},{... | collective-permute-start | bytes 393224 | tf_op jit(solution)/shard_map/ppermute | solution.py:315
  13.3 1.9 %shard_map.83 = bf16[8,80,256]{2,1,0:T(8,128)(2,1)} custom-call(bf16[512,896]{1,0:T(8,128)(2,1)S(1)} %bitcast.19, bf16[512,128]{1,0:T(8,128)(2,1)S(1)} %bitcast.24, bf16[224,256]{1,0:T(8,128)(2,1)S(1)} %shard_map.82.refs_0_, bf16[224,256]{1,0:T(8,128)(2,1)S(1)} %collective-permute-done.refs_1_, bf16[224,256]{1,0:T(8,128)(2,1)S(1)} %collective-permute-done.1.refs_2_, ...), custom_call_target="tpu_custom_call" | custom-call | flops 234881024 | bytes 917504 | tf_op jit(solution)/shard_map/pallas_call | solution.py:72
  15.2 4.6 %collective-permute-done.7 = bf16[512,128]{1,0:T(8,128)(2,1)S(1)} collective-permute-done((bf16[512,128]{1,0:T(8,128)(2,1)}, bf16[512,128]{1,0:T(8,128)(2,1)S(1)}, u32[]{:S(2)}, u32[]{:S(2)}) %collective-permute-start.7) | collective-permute-done | bytes 131104 | tf_op jit(solution)/shard_map/ppermute | solution.py:315
  20.7 1.5 %collective-permute-start.10 = (bf16[4,512,128]{2,1,0:T(8,128)(2,1)}, bf16[4,512,128]{2,1,0:T(8,128)(2,1)}, u32[]{:S(2)}, u32[]{:S(2)}) collective-permute-start(bf16[4,512,128]{2,1,0:T(8,128)(2,1)} %pad_maximum_fusion.refs_0_), channel_id=1, source_target_pairs={{0,1},{1,0},{2,3},{3,2},{4,5},{5,4},{6,7},{7,6},{8,9},{9,8},{10,11... | collective-permute-start | bytes 1572872 | tf_op jit(solution)/shard_map/ppermute | solution.py:315
  22.2 1.5 %collective-permute-start.12 = (bf16[4,512,128]{2,1,0:T(8,128)(2,1)}, bf16[4,512,128]{2,1,0:T(8,128)(2,1)}, u32[]{:S(2)}, u32[]{:S(2)}) collective-permute-start(bf16[4,512,128]{2,1,0:T(8,128)(2,1)} %pad_maximum_fusion.refs_0_), channel_id=1, source_target_pairs={{0,2},{1,3},{2,0},{3,1},{4,6},{5,7},{6,4},{7,5},{8,10},{9,11},{10,... | collective-permute-start | bytes 1572872 | tf_op jit(solution)/shard_map/ppermute | solution.py:315
  24.2 10.6 %collective-permute-done.14 = bf16[512,128]{1,0:T(8,128)(2,1)S(1)} collective-permute-done((bf16[512,128]{1,0:T(8,128)(2,1)S(1)}, bf16[512,128]{1,0:T(8,128)(2,1)S(1)}, u32[]{:S(2)}, u32[]{:S(2)}) %collective-permute-start.14) | collective-permute-done | bytes 131104 | tf_op jit(solution)/shard_map/ppermute | solution.py:315
  34.9 4.5 %collective-permute-start.15 = (bf16[512,128]{1,0:T(8,128)(2,1)S(1)}, bf16[512,128]{1,0:T(8,128)(2,1)S(1)}, u32[]{:S(2)}, u32[]{:S(2)}) collective-permute-start(bf16[512,128]{1,0:T(8,128)(2,1)S(1)} %collective-permute-done.14), channel_id=1, source_target_pairs={{0,8},{4,12},{8,0},{12,4},{16,24},{20,28},{24,16},{28,20},{1,9},{5... | collective-permute-start | bytes 393224 | tf_op jit(solution)/shard_map/ppermute | solution.py:315
  39.8 1.9 %collective-permute-start.17 = (bf16[512,128]{1,0:T(8,128)(2,1)S(1)}, bf16[512,128]{1,0:T(8,128)(2,1)S(1)}, u32[]{:S(2)}, u32[]{:S(2)}) collective-permute-start(bf16[512,128]{1,0:T(8,128)(2,1)S(1)} %collective-permute-done.14), channel_id=1, source_target_pairs={{0,24},{4,28},{8,16},{12,20},{16,8},{20,12},{24,0},{28,4},{1,25},{... | collective-permute-start | bytes 393224 | tf_op jit(solution)/shard_map/ppermute | solution.py:315
  41.7 3.4 %all-to-all-start = ((bf16[8,80,256]{2,1,0:T(8,128)(2,1)}), bf16[8,80,256]{2,1,0:T(8,128)(2,1)S(1)}, u32[]{:S(2)}, u32[]{:S(2)}) async-start(bf16[8,80,256]{2,1,0:T(8,128)(2,1)} %shard_map.83), calls=%async_computation | async-start | bytes 655360 | tf_op jit(solution)/shard_map/all_to_all | solution.py:324
  45.5 3.9 %collective-permute-done.16 = bf16[512,128]{1,0:T(8,128)(2,1)S(1)} collective-permute-done((bf16[512,128]{1,0:T(8,128)(2,1)S(1)}, bf16[512,128]{1,0:T(8,128)(2,1)S(1)}, u32[]{:S(2)}, u32[]{:S(2)}) %collective-permute-start.16) | collective-permute-done | bytes 131104 | tf_op jit(solution)/shard_map/ppermute | solution.py:315
  51.0 7.4 %all-to-all-done.y_ref = bf16[8,80,256]{2,1,0:T(8,128)(2,1)S(1)} async-done(((bf16[8,80,256]{2,1,0:T(8,128)(2,1)}), bf16[8,80,256]{2,1,0:T(8,128)(2,1)S(1)}, u32[]{:S(2)}, u32[]{:S(2)}) %all-to-all-start) | async-done | bytes 327712 | tf_op jit(solution)/shard_map/all_to_all | solution.py:324
  59.1 11.2 %shard_map.86 = bf16[8,64,256]{2,1,0:T(8,128)(2,1)} custom-call(bf16[8,80,256]{2,1,0:T(8,128)(2,1)} %copy-done.3, s32[8,8]{1,0:T(8,128)} %table_hbm.1, bf16[8,512,2048]{2,1,0:T(8,128)(2,1)} %exch_hbm.1, bf16[4,512,128]{2,1,0:T(8,128)(2,1)} %pad_maximum_fusion.refs_0_, bf16[4,512,128]{2,1,0:T(8,128)(2,1)} %collective-permute-done.9.refs_1_, ...), custom_call_target="tpu_custom_call" | custom-call | flops 17179869184 | bytes 6291456 | tf_op jit(solution)/shard_map/pallas_call | solution.py:178
  70.3 4.1 %all-to-all-start.1 = ((bf16[8,64,256]{2,1,0:T(8,128)(2,1)}), bf16[8,64,256]{2,1,0:T(8,128)(2,1)}, u32[]{:S(2)}, u32[]{:S(2)}) async-start(bf16[8,64,256]{2,1,0:T(8,128)(2,1)} %shard_map.86), calls=%async_computation.1 | async-start | bytes 524288 | tf_op jit(solution)/shard_map/all_to_all | solution.py:324
  75.4 1.6 %collective-permute-start.3 = (bf16[2,512]{1,0:T(2,128)(2,1)S(1)}, bf16[2,512]{1,0:T(2,128)(2,1)S(1)}, u32[]{:S(2)}, u32[]{:S(2)}) collective-permute-start(bf16[2,512]{1,0:T(2,128)(2,1)S(1)} %shard_map.84.refs_0_), channel_id=1, source_target_pairs={{0,1},{1,0},{2,3},{3,2},{4,5},{5,4},{6,7},{7,6},{8,9},{9,8},{10,11... | collective-permute-start | bytes 6152 | tf_op jit(solution)/shard_map/ppermute | solution.py:315
  77.4 1.5 %collective-permute-start.5 = (bf16[2,512]{1,0:T(2,128)(2,1)S(1)}, bf16[2,512]{1,0:T(2,128)(2,1)S(1)}, u32[]{:S(2)}, u32[]{:S(2)}) collective-permute-start(bf16[2,512]{1,0:T(2,128)(2,1)S(1)} %shard_map.84.refs_0_), channel_id=1, source_target_pairs={{0,3},{1,2},{2,1},{3,0},{4,7},{5,6},{6,5},{7,4},{8,11},{9,10},{10,... | collective-permute-start | bytes 6152 | tf_op jit(solution)/shard_map/ppermute | solution.py:315
  79.0 1.5 %collective-permute-done.4.refs_2_ = bf16[2,512]{1,0:T(2,128)(2,1)S(1)} collective-permute-done((bf16[2,512]{1,0:T(2,128)(2,1)S(1)}, bf16[2,512]{1,0:T(2,128)(2,1)S(1)}, u32[]{:S(2)}, u32[]{:S(2)}) %collective-permute-start.4) | collective-permute-done | bytes 2080 | tf_op jit(solution)/shard_map/ppermute | solution.py:315
  84.1 1.5 %shard_map.87 = (f32[224,256]{1,0:T(8,128)S(1)}, bf16[224,256]{1,0:T(8,128)(2,1)S(1)}, bf16[224,256]{1,0:T(8,128)(2,1)S(1)}, bf16[224,256]{1,0:T(8,128)(2,1)S(1)}) custom-call(f32[512,256]{1,0:T(8,128)S(1)} %shard_map.85.direct_ref, bf16[512,256]{1,0:T(8,128)(2,1)} %bitcast.15.z_ref, bf16[512,896]{1,0:T(8,128)(2,1)S(1)} %bitcast.20), custom_call_target="tpu_custom_call" | custom-call | flops 234881024 | bytes 917504 | tf_op jit(solution)/shard_map/pallas_call | solution.py:283
  85.6 1.6 %collective-permute-start.19 = (bf16[224,256]{1,0:T(8,128)(2,1)S(1)}, bf16[224,256]{1,0:T(8,128)(2,1)S(1)}, u32[]{:S(2)}, u32[]{:S(2)}) collective-permute-start(bf16[224,256]{1,0:T(8,128)(2,1)S(1)} %get-tuple-element.18), channel_id=1, source_target_pairs={{0,1},{1,0},{2,3},{3,2},{4,5},{5,4},{6,7},{7,6},{8,9},{9,8},{10,11... | collective-permute-start | bytes 344072 | tf_op jit(solution)/shard_map/ppermute | solution.py:315
  87.7 1.5 %collective-permute-start.21 = (bf16[224,256]{1,0:T(8,128)(2,1)S(1)}, bf16[224,256]{1,0:T(8,128)(2,1)S(1)}, u32[]{:S(2)}, u32[]{:S(2)}) collective-permute-start(bf16[224,256]{1,0:T(8,128)(2,1)S(1)} %get-tuple-element.20), channel_id=1, source_target_pairs={{0,3},{1,2},{2,1},{3,0},{4,7},{5,6},{6,5},{7,4},{8,11},{9,10},{10,... | collective-permute-start | bytes 344072 | tf_op jit(solution)/shard_map/ppermute | solution.py:315
  89.2 1.5 %collective-permute-done.19.refs_0_ = bf16[224,256]{1,0:T(8,128)(2,1)S(1)} collective-permute-done((bf16[224,256]{1,0:T(8,128)(2,1)S(1)}, bf16[224,256]{1,0:T(8,128)(2,1)S(1)}, u32[]{:S(2)}, u32[]{:S(2)}) %collective-permute-start.19) | collective-permute-done | bytes 114720 | tf_op jit(solution)/shard_map/ppermute | solution.py:315
  90.8 3.3 %collective-permute-done.20.refs_1_ = bf16[224,256]{1,0:T(8,128)(2,1)S(1)} collective-permute-done((bf16[224,256]{1,0:T(8,128)(2,1)S(1)}, bf16[224,256]{1,0:T(8,128)(2,1)S(1)}, u32[]{:S(2)}, u32[]{:S(2)}) %collective-permute-start.20) | collective-permute-done | bytes 114720 | tf_op jit(solution)/shard_map/ppermute | solution.py:315
  (56 shorter events, 16.1 us)
Async XLA Ops:
  1.0 9.2 %collective-permute-start = (bf16[224,256]{1,0:T(8,128)(2,1)S(1)}, bf16[224,256]{1,0:T(8,128)(2,1)S(1)}, u32[]{:S(2)}, u32[]{:S(2)}) collective-permute-start(bf16[224,256]{1,0:T(8,128)(2,1)S(1)} %shard_map.82.refs_0_), channel_id=1, source_target_pairs={{0,1},{1,0},{2,3},{3,2},{4,5},{5,4},{6,7},{7,6},{8,9},{9,8},{10,11... | collective-permute-start | bytes 344072 | tf_op jit(solution)/shard_map/ppermute | solution.py:315
  4.0 7.2 %collective-permute-start.1 = (bf16[224,256]{1,0:T(8,128)(2,1)S(1)}, bf16[224,256]{1,0:T(8,128)(2,1)S(1)}, u32[]{:S(2)}, u32[]{:S(2)}) collective-permute-start(bf16[224,256]{1,0:T(8,128)(2,1)S(1)} %shard_map.82.refs_0_), channel_id=1, source_target_pairs={{0,2},{1,3},{2,0},{3,1},{4,6},{5,7},{6,4},{7,5},{8,10},{9,11},{10,... | collective-permute-start | bytes 344072 | tf_op jit(solution)/shard_map/ppermute | solution.py:315
  5.5 5.7 %collective-permute-start.2 = (bf16[224,256]{1,0:T(8,128)(2,1)S(1)}, bf16[224,256]{1,0:T(8,128)(2,1)S(1)}, u32[]{:S(2)}, u32[]{:S(2)}) collective-permute-start(bf16[224,256]{1,0:T(8,128)(2,1)S(1)} %shard_map.82.refs_0_), channel_id=1, source_target_pairs={{0,3},{1,2},{2,1},{3,0},{4,7},{5,6},{6,5},{7,4},{8,11},{9,10},{10,... | collective-permute-start | bytes 344072 | tf_op jit(solution)/shard_map/ppermute | solution.py:315
  5.5 9.7 %collective-permute-start.6 = (bf16[512,128]{1,0:T(8,128)(2,1)}, bf16[512,128]{1,0:T(8,128)(2,1)S(1)}, u32[]{:S(2)}, u32[]{:S(2)}) collective-permute-start(bf16[512,128]{1,0:T(8,128)(2,1)} %bitcast.21), channel_id=1, source_target_pairs={{0,8},{4,12},{8,0},{12,4},{16,24},{20,28},{24,16},{28,20},{1,9},{5... | collective-permute-start | bytes 393224 | tf_op jit(solution)/shard_map/ppermute | solution.py:315
  7.6 12.3 %collective-permute-start.7 = (bf16[512,128]{1,0:T(8,128)(2,1)}, bf16[512,128]{1,0:T(8,128)(2,1)S(1)}, u32[]{:S(2)}, u32[]{:S(2)}) collective-permute-start(bf16[512,128]{1,0:T(8,128)(2,1)} %bitcast.22), channel_id=1, source_target_pairs={{0,16},{4,20},{8,24},{12,28},{16,0},{20,4},{24,8},{28,12},{1,17},{... | collective-permute-start | bytes 393224 | tf_op jit(solution)/shard_map/ppermute | solution.py:315
  10.2 9.7 %collective-permute-start.8 = (bf16[512,128]{1,0:T(8,128)(2,1)}, bf16[512,128]{1,0:T(8,128)(2,1)S(1)}, u32[]{:S(2)}, u32[]{:S(2)}) collective-permute-start(bf16[512,128]{1,0:T(8,128)(2,1)} %bitcast.23), channel_id=1, source_target_pairs={{0,24},{4,28},{8,16},{12,20},{16,8},{20,12},{24,0},{28,4},{1,25},{... | collective-permute-start | bytes 393224 | tf_op jit(solution)/shard_map/ppermute | solution.py:315
  20.7 29.6 %collective-permute-start.10 = (bf16[4,512,128]{2,1,0:T(8,128)(2,1)}, bf16[4,512,128]{2,1,0:T(8,128)(2,1)}, u32[]{:S(2)}, u32[]{:S(2)}) collective-permute-start(bf16[4,512,128]{2,1,0:T(8,128)(2,1)} %pad_maximum_fusion.refs_0_), channel_id=1, source_target_pairs={{0,1},{1,0},{2,3},{3,2},{4,5},{5,4},{6,7},{7,6},{8,9},{9,8},{10,11... | collective-permute-start | bytes 1572872 | tf_op jit(solution)/shard_map/ppermute | solution.py:315
  22.2 28.6 %collective-permute-start.12 = (bf16[4,512,128]{2,1,0:T(8,128)(2,1)}, bf16[4,512,128]{2,1,0:T(8,128)(2,1)}, u32[]{:S(2)}, u32[]{:S(2)}) collective-permute-start(bf16[4,512,128]{2,1,0:T(8,128)(2,1)} %pad_maximum_fusion.refs_0_), channel_id=1, source_target_pairs={{0,2},{1,3},{2,0},{3,1},{4,6},{5,7},{6,4},{7,5},{8,10},{9,11},{10,... | collective-permute-start | bytes 1572872 | tf_op jit(solution)/shard_map/ppermute | solution.py:315
  23.7 11.1 %collective-permute-start.14 = (bf16[512,128]{1,0:T(8,128)(2,1)S(1)}, bf16[512,128]{1,0:T(8,128)(2,1)S(1)}, u32[]{:S(2)}, u32[]{:S(2)}) collective-permute-start(bf16[512,128]{1,0:T(8,128)(2,1)S(1)} %bitcast.25), channel_id=1, source_target_pairs={{0,3},{1,2},{2,1},{3,0},{4,7},{5,6},{6,5},{7,4},{8,11},{9,10},{10,... | collective-permute-start | bytes 393224 | tf_op jit(solution)/shard_map/ppermute | solution.py:315
  34.9 10.3 %collective-permute-start.15 = (bf16[512,128]{1,0:T(8,128)(2,1)S(1)}, bf16[512,128]{1,0:T(8,128)(2,1)S(1)}, u32[]{:S(2)}, u32[]{:S(2)}) collective-permute-start(bf16[512,128]{1,0:T(8,128)(2,1)S(1)} %collective-permute-done.14), channel_id=1, source_target_pairs={{0,8},{4,12},{8,0},{12,4},{16,24},{20,28},{24,16},{28,20},{1,9},{5... | collective-permute-start | bytes 393224 | tf_op jit(solution)/shard_map/ppermute | solution.py:315
  39.3 10.1 %collective-permute-start.16 = (bf16[512,128]{1,0:T(8,128)(2,1)S(1)}, bf16[512,128]{1,0:T(8,128)(2,1)S(1)}, u32[]{:S(2)}, u32[]{:S(2)}) collective-permute-start(bf16[512,128]{1,0:T(8,128)(2,1)S(1)} %collective-permute-done.14), channel_id=1, source_target_pairs={{0,16},{4,20},{8,24},{12,28},{16,0},{20,4},{24,8},{28,12},{1,17},{... | collective-permute-start | bytes 393224 | tf_op jit(solution)/shard_map/ppermute | solution.py:315
  39.8 9.6 %collective-permute-start.17 = (bf16[512,128]{1,0:T(8,128)(2,1)S(1)}, bf16[512,128]{1,0:T(8,128)(2,1)S(1)}, u32[]{:S(2)}, u32[]{:S(2)}) collective-permute-start(bf16[512,128]{1,0:T(8,128)(2,1)S(1)} %collective-permute-done.14), channel_id=1, source_target_pairs={{0,24},{4,28},{8,16},{12,20},{16,8},{20,12},{24,0},{28,4},{1,25},{... | collective-permute-start | bytes 393224 | tf_op jit(solution)/shard_map/ppermute | solution.py:315
  41.7 16.6 %all-to-all-start = ((bf16[8,80,256]{2,1,0:T(8,128)(2,1)}), bf16[8,80,256]{2,1,0:T(8,128)(2,1)S(1)}, u32[]{:S(2)}, u32[]{:S(2)}) async-start(bf16[8,80,256]{2,1,0:T(8,128)(2,1)} %shard_map.83), calls=%async_computation | async-start | bytes 655360 | tf_op jit(solution)/shard_map/all_to_all | solution.py:324
  45.1 5.8 %collective-permute-start.9 = (bf16[4,512,128]{2,1,0:T(8,128)(2,1)}, bf16[4,512,128]{2,1,0:T(8,128)(2,1)}, u32[]{:S(2)}, u32[]{:S(2)}) collective-permute-start(bf16[4,512,128]{2,1,0:T(8,128)(2,1)} %pad_maximum_fusion.refs_0_), channel_id=1, source_target_pairs={{0,4},{4,0},{8,12},{12,8},{16,20},{20,16},{24,28},{28,24},{1,5},{5... | collective-permute-start | bytes 1572872 | tf_op jit(solution)/shard_map/ppermute | solution.py:315
  50.3 8.0 %collective-permute-start.18 = (bf16[4,512,128]{2,1,0:T(8,128)(2,1)}, bf16[4,512,128]{2,1,0:T(8,128)(2,1)}, u32[]{:S(2)}, u32[]{:S(2)}) collective-permute-start(bf16[4,512,128]{2,1,0:T(8,128)(2,1)} %pad_maximum_fusion.1.refs_6_), channel_id=1, source_target_pairs={{0,4},{4,0},{8,12},{12,8},{16,20},{20,16},{24,28},{28,24},{1,5},{5... | collective-permute-start | bytes 1572872 | tf_op jit(solution)/shard_map/ppermute | solution.py:315
  50.4 7.9 %collective-permute-start.11 = (bf16[4,512,128]{2,1,0:T(8,128)(2,1)}, bf16[4,512,128]{2,1,0:T(8,128)(2,1)}, u32[]{:S(2)}, u32[]{:S(2)}) collective-permute-start(bf16[4,512,128]{2,1,0:T(8,128)(2,1)} %collective-permute-done.10.refs_2_), channel_id=1, source_target_pairs={{0,4},{4,0},{8,12},{12,8},{16,20},{20,16},{24,28},{28,24},{1,5},{5... | collective-permute-start | bytes 1572872 | tf_op jit(solution)/shard_map/ppermute | solution.py:315
  50.9 7.5 %collective-permute-start.13 = (bf16[4,512,128]{2,1,0:T(8,128)(2,1)}, bf16[4,512,128]{2,1,0:T(8,128)(2,1)}, u32[]{:S(2)}, u32[]{:S(2)}) collective-permute-start(bf16[4,512,128]{2,1,0:T(8,128)(2,1)} %collective-permute-done.12.refs_4_), channel_id=1, source_target_pairs={{0,4},{4,0},{8,12},{12,8},{16,20},{20,16},{24,28},{28,24},{1,5},{5... | collective-permute-start | bytes 1572872 | tf_op jit(solution)/shard_map/ppermute | solution.py:315
  70.3 13.8 %all-to-all-start.1 = ((bf16[8,64,256]{2,1,0:T(8,128)(2,1)}), bf16[8,64,256]{2,1,0:T(8,128)(2,1)}, u32[]{:S(2)}, u32[]{:S(2)}) async-start(bf16[8,64,256]{2,1,0:T(8,128)(2,1)} %shard_map.86), calls=%async_computation.1 | async-start | bytes 524288 | tf_op jit(solution)/shard_map/all_to_all | solution.py:324
  75.4 3.7 %collective-permute-start.3 = (bf16[2,512]{1,0:T(2,128)(2,1)S(1)}, bf16[2,512]{1,0:T(2,128)(2,1)S(1)}, u32[]{:S(2)}, u32[]{:S(2)}) collective-permute-start(bf16[2,512]{1,0:T(2,128)(2,1)S(1)} %shard_map.84.refs_0_), channel_id=1, source_target_pairs={{0,1},{1,0},{2,3},{3,2},{4,5},{5,4},{6,7},{7,6},{8,9},{9,8},{10,11... | collective-permute-start | bytes 6152 | tf_op jit(solution)/shard_map/ppermute | solution.py:315
  76.9 3.6 %collective-permute-start.4 = (bf16[2,512]{1,0:T(2,128)(2,1)S(1)}, bf16[2,512]{1,0:T(2,128)(2,1)S(1)}, u32[]{:S(2)}, u32[]{:S(2)}) collective-permute-start(bf16[2,512]{1,0:T(2,128)(2,1)S(1)} %shard_map.84.refs_0_), channel_id=1, source_target_pairs={{0,2},{1,3},{2,0},{3,1},{4,6},{5,7},{6,4},{7,5},{8,10},{9,11},{10,... | collective-permute-start | bytes 6152 | tf_op jit(solution)/shard_map/ppermute | solution.py:315
  77.4 4.5 %collective-permute-start.5 = (bf16[2,512]{1,0:T(2,128)(2,1)S(1)}, bf16[2,512]{1,0:T(2,128)(2,1)S(1)}, u32[]{:S(2)}, u32[]{:S(2)}) collective-permute-start(bf16[2,512]{1,0:T(2,128)(2,1)S(1)} %shard_map.84.refs_0_), channel_id=1, source_target_pairs={{0,3},{1,2},{2,1},{3,0},{4,7},{5,6},{6,5},{7,4},{8,11},{9,10},{10,... | collective-permute-start | bytes 6152 | tf_op jit(solution)/shard_map/ppermute | solution.py:315
  85.6 5.2 %collective-permute-start.19 = (bf16[224,256]{1,0:T(8,128)(2,1)S(1)}, bf16[224,256]{1,0:T(8,128)(2,1)S(1)}, u32[]{:S(2)}, u32[]{:S(2)}) collective-permute-start(bf16[224,256]{1,0:T(8,128)(2,1)S(1)} %get-tuple-element.18), channel_id=1, source_target_pairs={{0,1},{1,0},{2,3},{3,2},{4,5},{5,4},{6,7},{7,6},{8,9},{9,8},{10,11... | collective-permute-start | bytes 344072 | tf_op jit(solution)/shard_map/ppermute | solution.py:315
  87.1 6.9 %collective-permute-start.20 = (bf16[224,256]{1,0:T(8,128)(2,1)S(1)}, bf16[224,256]{1,0:T(8,128)(2,1)S(1)}, u32[]{:S(2)}, u32[]{:S(2)}) collective-permute-start(bf16[224,256]{1,0:T(8,128)(2,1)S(1)} %get-tuple-element.19), channel_id=1, source_target_pairs={{0,2},{1,3},{2,0},{3,1},{4,6},{5,7},{6,4},{7,5},{8,10},{9,11},{10,... | collective-permute-start | bytes 344072 | tf_op jit(solution)/shard_map/ppermute | solution.py:315
  87.7 6.4 %collective-permute-start.21 = (bf16[224,256]{1,0:T(8,128)(2,1)S(1)}, bf16[224,256]{1,0:T(8,128)(2,1)S(1)}, u32[]{:S(2)}, u32[]{:S(2)}) collective-permute-start(bf16[224,256]{1,0:T(8,128)(2,1)S(1)} %get-tuple-element.20), channel_id=1, source_target_pairs={{0,3},{1,2},{2,1},{3,0},{4,7},{5,6},{6,5},{7,4},{8,11},{9,10},{10,... | collective-permute-start | bytes 344072 | tf_op jit(solution)/shard_map/ppermute | solution.py:315
  (11 other events, 149.7 us)
